TPU v7x, 32 devices: a whole 2x2x4 slice. The times are simulated.
32 devices in a mesh: row: 8 (over z, x), col: 4 (over y, core).
Axes of the slice: x: 2, y: 2, z: 4, core: 2. Of those that a mesh axis runs over, the one named last changes fastest.
Arguments:
- lower: bfloat16 [8, 3, 512, 2, 512], P('row', None, None, None, 'col'), as said below
- rhs: bfloat16 [8, 3, 512, 8192], P('row', None, None, 'col'), may hold values from -6 to 6
- tile_map: int32 [16], replicated, may hold values from 0 to 15, each once
Outputs:
- overwritten: bfloat16 [8, 3, 512, 8192], P('row', None, None, 'col')
Inputs may be any that keep to these rules, and one draw needn't show every extreme that they name: tile_map is a permutation of 0 to 15. lower[0, 0, :, 0, :] and lower[1, 0, :, 1, :] are lower triangular with diagonal entries between 2 and 3; lower[0, 0, :, 1, :] is zero.
All inputs are finite; a program needn't handle non-finite values.
Results may differ from a plain program's by a relative error of at most 0.0032.
Values may be sent and summed in bfloat16 or wider, within the bound.
A program may use at most 128 MiB of HBM per device.

v0:
```python
import jax
import jax.numpy as jnp
from jax import lax
from jax.sharding import PartitionSpec as P


def from_root(value, axis, source):
    kept = jnp.where(lax.axis_index(axis) == source, value, 0).astype(value.dtype)
    return lax.psum(kept, axis)


def reorder(block, tile_map, tile):
    shape = block.shape
    tiles = block.reshape(shape[:-1] + (shape[-1] // tile, tile))
    return jnp.take(tiles, tile_map, axis=3).reshape(shape)


def body(lower, rhs, tile_map):
    tile = lower.shape[2]
    here = lax.axis_index("row")
    whole = lax.all_gather(lower, "col", axis=4, tiled=True)
    panels = whole[0]
    rows = panels.shape[0] * tile
    rhs = lax.all_to_all(
        reorder(
            lax.all_to_all(rhs, "col", split_axis=2, concat_axis=3, tiled=True), tile_map, tile
        ),
        "col",
        split_axis=3,
        concat_axis=2,
        tiled=True,
    )
    work = rhs[0].astype(jnp.float32)
    identity = jnp.eye(tile, dtype=jnp.float32)
    solved_rows = []
    for panel in range(2):
        mine = jnp.where(
            here == panel, jnp.tril(panels[0, :, panel, :].astype(jnp.float32)), identity
        )
        local = jax.scipy.linalg.solve_triangular(mine, work[0], lower=True).astype(jnp.bfloat16)
        solved = from_root(local, "row", panel)
        flat = panels[:, :, panel, :].reshape(rows, tile)
        work = work - jnp.dot(flat, solved, preferred_element_type=jnp.float32).reshape(work.shape)
        solved_rows.append(solved)
    first, second = (solved_rows[0], solved_rows[1])
    result = work.astype(jnp.bfloat16)
    leading = jnp.where(here == 0, first, jnp.where(here == 1, second, result[0]))
    result = result.at[0].set(leading)[None]
    return result


def solution(mesh):
    placed = (P("row", None, None, None, "col"), P("row", None, None, "col"), P())
    return jax.shard_map(
        body, mesh=mesh, in_specs=placed, out_specs=P("row", None, None, "col"), check_vma=False
    )
```

profile of v0, /device:TPU:0, one launch (start us, length us, event | category | flops | bytes accessed | tf_op | source)
XLA Modules:
  0.0 617.3 jit_solution(11113632346526701513)
XLA Ops:
  6.5 11.4 %copy.15 = bf16[1,3,512,2048]{3,1,0,2:T(4,128)(2,1)} copy(bf16[1,3,512,2048]{3,2,1,0:T(8,128)(2,1)} %param.8) | data formatting | bytes 12582912 | tf_op args[1]
  17.9 5.8 all-to-all-start
  25.1 109.3 %all-to-all-done = bf16[1,3,512,2048]{3,1,0,2:T(4,128)(2,1)} async-done(((bf16[1,3,512,2048]{3,1,0,2:T(4,128)(2,1)}), bf16[1,3,512,2048]{3,1,0,2:T(4,128)(2,1)}, u32[]{:S(2)}, u32[]{:S(2)}) %all-to-all-start) | async-done | bytes 6291488 | tf_op jit(solution)/shard_map/all_to_all | solution.py:26
  134.4 10.6 %copy.16 = bf16[1,3,512,2048]{3,2,1,0:T(8,128)(2,1)} copy(bf16[1,3,512,2048]{3,1,0,2:T(4,128)(2,1)} %all-to-all-done) | data formatting | bytes 12582912 | tf_op jit(solution)/shard_map/all_to_all | solution.py:26
  145.0 8.7 %copy.17 = bf16[1,3,128,4,2048]{2,4,3,1,0:T(8,128)(2,1)} copy(bf16[1,3,128,4,2048]{4,2,3,1,0:T(8,128)(2,1)} %bitcast.121) | data formatting | bytes 12582912 | tf_op jit(solution)/shard_map/all_to_all | solution.py:26
  153.7 8.6 %copy.18 = bf16[3,128,16,512]{3,1,2,0:T(8,128)(2,1)} copy(bf16[3,128,16,512]{1,3,2,0:T(8,128)(2,1)} %bitcast.122) | data formatting | bytes 12582912 | tf_op jit(solution)/shard_map/reshape | solution.py:14
  162.3 6.4 %gather_fusion = bf16[16,3,128,512]{3,2,1,0:T(8,128)(2,1)} fusion(bf16[3,128,16,512]{3,1,2,0:T(8,128)(2,1)} %copy.18, s32[1024]{0:T(1024)S(1)} %pad_clamp_fusion), kind=kCustom, calls=%fused_computation | custom fusion | bytes 12582976 | tf_op jit(solution)/shard_map/jit(_take)/gather | solution.py:15
  168.7 8.6 %copy.19 = bf16[3,128,16,512]{1,3,2,0:T(8,128)(2,1)} copy(bf16[3,128,16,512]{3,1,0,2:T(8,128)(2,1)} %bitcast.120) | data formatting | bytes 12582912 | tf_op jit(solution)/shard_map/jit(_take)/gather | solution.py:15
  177.3 4.1 bitcast_select_fusion
  181.4 39.9 %copy.20 = bf16[1,3,128,8192]{2,1,0,3:T(4,128)(2,1)} copy(bf16[1,3,128,8192]{2,3,1,0:T(8,128)(2,1)S(1)} %bitcast_select_fusion) | data formatting | bytes 12582912 | tf_op jit(solution)/shard_map/jit(_take)/select_n | solution.py:15
  221.3 5.7 all-to-all-start.1
  227.3 2.5 fusion.35
  229.8 8.1 %while.5 = (s32[]{:T(128)}, f32[512,512]{1,0:T(8,128)S(1)}, s32[4,2]{0,1:T(2,128)S(1)}, f32[4,128,128]{2,1,0:T(8,128)S(1)}, s32[]{:T(128)}) while((s32[]{:T(128)}, f32[512,512]{1,0:T(8,128)S(1)}, s32[4,2]{0,1:T(2,128)S(1)}, f32[4,128,128]{2,1,0:T(8,128)S(1)}, s32[]{:T(128)}) %tuple.41), condition=%wide.while_cond.1, body=%wide.while_body.1.sunk | while | flops 2 | bytes 131189 | solution.py:40
  238.0 39.3 %custom-call.4 = f32[4,128,128]{1,2,0:T(8,128)S(1)} custom-call(f32[4,128,128]{2,1,0:T(8,128)S(1)} %get-tuple-element.32), custom_call_target="InvertDiagBlocksLowerTriangular" | custom-call | tf_op jit(solution)/shard_map/jit(_solve_triangular)/triangular_solve | solution.py:40
  277.3 42.9 %all-to-all-done.1 = bf16[1,3,128,8192]{2,1,0,3:T(4,128)(2,1)} async-done(((bf16[1,3,128,8192]{2,1,0,3:T(4,128)(2,1)}), bf16[1,3,128,8192]{2,1,0,3:T(4,128)(2,1)}, u32[]{:S(2)}, u32[]{:S(2)}) %all-to-all-start.1) | async-done | bytes 6291488 | tf_op jit(solution)/shard_map/all_to_all | solution.py:24
  320.2 4.3 copy.21
  325.6 4.6 copy-done.1
  332.4 5.4 copy.24
  337.9 2.4 fusion.38
  346.9 3.0 fusion.18
  352.8 11.8 %while.6 = (s32[]{:T(128)}, f32[512,512]{1,0:T(8,128)}, s32[4,2]{0,1:T(2,128)S(1)}, f32[4,128,128]{2,1,0:T(8,128)S(1)}, s32[]{:T(128)}) while((s32[]{:T(128)}, f32[512,512]{1,0:T(8,128)}, s32[4,2]{0,1:T(2,128)S(1)}, f32[4,128,128]{2,1,0:T(8,128)S(1)}, s32[]{:T(128)}) %tuple.53), condition=%wide.while_cond.1.clone, body=%wide.while_body.1.clone.sunk | while | flops 2 | bytes 131189 | solution.py:40
  365.3 40.1 %custom-call.5 = f32[4,128,128]{1,2,0:T(8,128)S(1)} custom-call(f32[4,128,128]{2,1,0:T(8,128)} %copy-done.11), custom_call_target="InvertDiagBlocksLowerTriangular" | custom-call | tf_op jit(solution)/shard_map/jit(_solve_triangular)/triangular_solve | solution.py:40
  407.3 12.8 %copy.22 = f32[1,3,4,128,2048]{4,3,2,1,0:T(8,128)} copy(f32[1,3,4,128,2048]{3,4,2,1,0:T(8,128)} %copy-done.1) | data formatting | bytes 25165824 | tf_op jit(solution)/shard_map/convert_element_type | solution.py:33
  420.0 36.3 %all-reduce.3.cloned.1.call-done = bf16[512,2048]{1,0:T(8,128)(2,1)} async-done(((bf16[512,2048]{1,0:T(8,128)(2,1)}), bf16[512,2048]{1,0:T(8,128)(2,1)}) %all-reduce.3.cloned.1.call-update) | async-done | bytes 2097168 | tf_op jit(solution)/shard_map/psum | solution.py:9
  456.3 5.2 fusion.59
  461.5 6.9 %sub.25 = f32[3,512,2048]{2,1,0:T(8,128)} subtract(f32[3,512,2048]{2,1,0:T(8,128)S(1)} %bitcast.117, f32[3,512,2048]{2,1,0:T(8,128)S(1)} %bitcast.118) | non-fusion elementwise | flops 3145728 | bytes 37748736 | tf_op jit(solution)/shard_map/sub | solution.py:43
  469.8 2.5 slice_bitcast_fusion
  479.4 3.0 fusion.15
  485.2 101.8 %all-reduce.5.cloned.1.call-done = bf16[512,2048]{1,0:T(8,128)(2,1)} async-done(((bf16[512,2048]{1,0:T(8,128)(2,1)}), bf16[512,2048]{1,0:T(8,128)(2,1)}) %all-reduce.5.cloned.1.call-update) | async-done | bytes 2097168 | tf_op jit(solution)/shard_map/psum | solution.py:9
  587.0 5.1 fusion.60
  592.1 13.4 %fusion.1 = bf16[1,3,512,2048]{3,2,1,0:T(8,128)(2,1)} fusion(f32[1,3,512,2048]{3,2,1,0:T(8,128)S(1)} %bitcast.124, f32[1,3,512,2048]{3,2,1,0:T(8,128)} %bitcast.119, f32[1,3,4,128,2048]{4,3,2,1,0:T(8,128)} %copy.22), kind=kLoop, calls=%fused_computation.8 | loop fusion | flops 9437184 | bytes 44040192 | tf_op jit(solution)/shard_map/convert_element_type | solution.py:46
  605.5 5.0 fusion.27
  (82 shorter events, 47.8 us)
Async XLA Ops:
  17.9 6.0 copy-start.10
  17.9 7.0 %copy-start.12 = (s32[16]{0:T(128)S(1)}, s32[16]{0:T(128)}, u32[]{:S(2)}) copy-start(s32[16]{0:T(128)} %param.9) | copy-start | bytes 196
  17.9 116.5 %all-to-all-start = ((bf16[1,3,512,2048]{3,1,0,2:T(4,128)(2,1)}), bf16[1,3,512,2048]{3,1,0,2:T(4,128)(2,1)}, u32[]{:S(2)}, u32[]{:S(2)}) async-start(bf16[1,3,512,2048]{3,1,0,2:T(4,128)(2,1)} %copy.15), calls=%async_computation | async-start | bytes 16777216 | tf_op jit(solution)/shard_map/all_to_all | solution.py:26
  23.7 203.6 %all-gather.2.cloned.1.call-start = ((), (), s32[]{:S(2)}) async-start(), calls=%async_computation.2 | async-start | bytes 3932160 | tf_op jit(solution)/shard_map/all_gather | solution.py:21
  221.3 98.8 %all-to-all-start.1 = ((bf16[1,3,128,8192]{2,1,0,3:T(4,128)(2,1)}), bf16[1,3,128,8192]{2,1,0,3:T(4,128)(2,1)}, u32[]{:S(2)}, u32[]{:S(2)}) async-start(bf16[1,3,128,8192]{2,1,0,3:T(4,128)(2,1)} %copy.20), calls=%async_computation.1 | async-start | bytes 16777216 | tf_op jit(solution)/shard_map/all_to_all | solution.py:24
  227.0 229.3 %all-reduce.3.cloned.1.call-start = ((), (), s32[]{:S(2)}) async-start(), calls=%async_computation.3 | async-start | bytes 4194304 | tf_op jit(solution)/shard_map/psum | solution.py:9
  237.9 39.3 %copy-start.5 = (f32[512,512]{1,0:T(8,128)}, f32[512,512]{1,0:T(8,128)S(1)}, u32[]{:S(2)}) copy-start(f32[512,512]{1,0:T(8,128)S(1)} %get-tuple-element.161) | copy-start | bytes 3145732
  325.6 4.6 copy-start.1
  337.9 5.8 copy-start.3
  350.9 54.5 %copy-start.4 = (bf16[1,3,512,2,512]{4,2,3,1,0:T(8,128)(2,1)S(1)}, bf16[1,3,512,2,512]{4,2,3,1,0:T(8,128)(2,1)}, u32[]{:S(2)}) copy-start(bf16[1,3,512,2,512]{4,2,3,1,0:T(8,128)(2,1)} %all-gather.2.cloned.1.call-done) | copy-start | bytes 9437188
  352.7 234.3 %all-reduce.5.cloned.1.call-start = ((), (), s32[]{:S(2)}) async-start(), calls=%async_computation.4 | async-start | bytes 4194304 | tf_op jit(solution)/shard_map/psum | solution.py:9
  364.6 0.7 copy-start.11
  407.3 49.0 %copy-start.9 = (bf16[3,512,1,512]{3,1,2,0:T(8,128)(2,1)S(1)}, bf16[3,512,1,512]{3,1,2,0:T(8,128)(2,1)}, u32[]{:S(2)}) copy-start(bf16[3,512,1,512]{3,1,2,0:T(8,128)(2,1)} %get-tuple-element.56) | copy-start | bytes 4718596
  456.3 5.2 copy-start
  461.5 8.3 %copy-start.2 = (f32[2048,1536]{0,1:T(8,128)}, f32[2048,1536]{0,1:T(8,128)S(1)}, u32[]{:S(2)}) copy-start(f32[2048,1536]{0,1:T(8,128)S(1)} %fusion.59) | copy-start | bytes 37748740
  483.4 103.6 %copy-start.8 = (bf16[3,512,1,512]{3,1,2,0:T(8,128)(2,1)S(1)}, bf16[3,512,1,512]{3,1,2,0:T(8,128)(2,1)}, u32[]{:S(2)}) copy-start(bf16[3,512,1,512]{3,1,2,0:T(8,128)(2,1)} %get-tuple-element.57) | copy-start | bytes 4718596
  592.1 13.4 %copy-start.6 = (bf16[512,2048]{1,0:T(8,128)(2,1)S(1)}, bf16[512,2048]{1,0:T(8,128)(2,1)}, u32[]{:S(2)}) copy-start(bf16[512,2048]{1,0:T(8,128)(2,1)} %all-reduce.3.cloned.1.call-done) | copy-start | bytes 6291460
  592.1 13.4 %copy-start.7 = (bf16[512,2048]{1,0:T(8,128)(2,1)S(1)}, bf16[512,2048]{1,0:T(8,128)(2,1)}, u32[]{:S(2)}) copy-start(bf16[512,2048]{1,0:T(8,128)(2,1)} %all-reduce.5.cloned.1.call-done) | copy-start | bytes 6291460
Sparse Core Ops, SparseCore 0:
  26.0 49.0 all-gather.1
  352.8 103.3 all-reduce.2
  485.4 101.5 all-reduce.4
where the time goes:
time: 624 us; the launch traced here: 617 us
  waiting for transfers between devices  290 us (46%)
  local copies, waits for them, and re-layouts  150 us (24%)
  other arithmetic  116 us (19%)
  matrix products  34.4 us (6%)
  between operations  13.7 us (2%)
  starting transfers between devices  12 us (2%)
    psum x2, waiting for transfers between devices, from_root(): return lax.psum(kept, axis)  138 us
    all_to_all x1, waiting for transfers between devices, body(): lax.all_to_all(rhs, 'col', split_axis=2, concat_axis=3, tiled=True)  109 us
    another operation x4, other arithmetic, body(): jax.scipy.linalg.solve_triangular(mine, work[0], lower=True)  81.9 us
    all_to_all x1, waiting for transfers between devices, body(): lax.all_to_all(reorder(lax.all_to_all(rhs, 'col', split_axis=2, concat_ax...  42.9 us
    select_n x1, local copies, waits for them, and re-layouts, reorder(): return jnp.take(tiles, tile_map, axis=3).reshape(shape)  39.9 us
    another operation x14, matrix products, body(): jax.scipy.linalg.solve_triangular(mine, work[0], lower=True)  24.1 us
    another operation x27, local copies, waits for them, and re-layouts, body(): jax.scipy.linalg.solve_triangular(mine, work[0], lower=True)  19.4 us
    all_to_all x2, local copies, waits for them, and re-layouts, body(): lax.all_to_all(rhs, 'col', split_axis=2, concat_axis=3, tiled=True)  19.3 us
  transfers between devices with their start and end apart: 5, of which 4 were waited for; matrix products, arithmetic and copies ran while one was open for 33% of the time, Pallas kernels for 0%

commit v1 on v0

--- a/solution.py
+++ b/solution.py
@@ -6,7 +6,7 @@
 
 def from_root(value, axis, source):
     kept = jnp.where(lax.axis_index(axis) == source, value, 0).astype(value.dtype)
-    return lax.psum(kept, axis)
+    return jnp.sum(lax.all_gather(kept, axis), axis=0)
 
 
 def reorder(block, tile_map, tile):

time: 624 us -> 892 us (1.43)
  waiting for transfers between devices: 290 us -> 540 us
  other arithmetic: 116 us -> 135 us
    all_gather x0 -> x2, waiting for transfers between devices: none -> 387 us  [from_root(): return jnp.sum(lax.all_gather(kept, axis), axis=0)]
    psum x2 -> x0, waiting for transfers between devices: 138 us -> none  [from_root(): return lax.psum(kept, axis)]
    reduce_sum x0 -> x2, other arithmetic: none -> 20.4 us  [from_root(): return jnp.sum(lax.all_gather(kept, axis), axis=0)]
    unnamed x30 -> x24, local copies, waits for them, and re-layouts: 19.1 us -> 19.3 us
  transfers between devices with their start and end apart: 5 -> 5, of which waited for: 4 -> 4; matrix products, arithmetic and copies ran while one was open for 33% -> 23% of each run, Pallas kernels for 0% -> 0%
where the time goes in v1:
time: 892 us; the launch traced here: 886 us
  waiting for transfers between devices  540 us (61%)
  local copies, waits for them, and re-layouts  150 us (17%)
  other arithmetic  135 us (15%)
  matrix products  34.7 us (4%)
  between operations  13.7 us (2%)
  starting transfers between devices  11.9 us (1%)
    all_gather x2, waiting for transfers between devices, from_root(): return jnp.sum(lax.all_gather(kept, axis), axis=0)  387 us
    all_to_all x1, waiting for transfers between devices, body(): lax.all_to_all(rhs, 'col', split_axis=2, concat_axis=3, tiled=True)  109 us
    another operation x4, other arithmetic, body(): jax.scipy.linalg.solve_triangular(mine, work[0], lower=True)  82 us
    all_to_all x1, waiting for transfers between devices, body(): lax.all_to_all(reorder(lax.all_to_all(rhs, 'col', split_axis=2, concat_ax...  43.3 us
    select_n x1, local copies, waits for them, and re-layouts, reorder(): return jnp.take(tiles, tile_map, axis=3).reshape(shape)  39.9 us
    another operation x14, matrix products, body(): jax.scipy.linalg.solve_triangular(mine, work[0], lower=True)  24.1 us
    reduce_sum x2, other arithmetic, from_root(): return jnp.sum(lax.all_gather(kept, axis), axis=0)  20.4 us
    unnamed x24, local copies, waits for them, and re-layouts  19.3 us
  transfers between devices with their start and end apart: 5, of which 4 were waited for; matrix products, arithmetic and copies ran while one was open for 23% of the time, Pallas kernels for 0%

profile of v1, /device:TPU:0, one launch (start us, length us, event | category | flops | bytes accessed | tf_op | source)
XLA Modules:
  0.0 885.7 jit_solution(9247484687984651827)
XLA Ops:
  6.5 11.4 %copy.14 = bf16[1,3,512,2048]{3,1,0,2:T(4,128)(2,1)} copy(bf16[1,3,512,2048]{3,2,1,0:T(8,128)(2,1)} %param.8) | data formatting | bytes 12582912 | tf_op args[1]
  17.9 5.8 all-to-all-start
  25.1 109.4 %all-to-all-done = bf16[1,3,512,2048]{3,1,0,2:T(4,128)(2,1)} async-done(((bf16[1,3,512,2048]{3,1,0,2:T(4,128)(2,1)}), bf16[1,3,512,2048]{3,1,0,2:T(4,128)(2,1)}, u32[]{:S(2)}, u32[]{:S(2)}) %all-to-all-start) | async-done | bytes 6291488 | tf_op jit(solution)/shard_map/all_to_all | solution.py:26
  134.4 10.6 %copy.15 = bf16[1,3,512,2048]{3,2,1,0:T(8,128)(2,1)} copy(bf16[1,3,512,2048]{3,1,0,2:T(4,128)(2,1)} %all-to-all-done) | data formatting | bytes 12582912 | tf_op jit(solution)/shard_map/all_to_all | solution.py:26
  145.0 8.6 copy.16
  153.7 8.6 copy.17
  162.3 6.4 gather_fusion
  168.7 8.6 copy.18
  177.3 4.1 bitcast_select_fusion
  181.4 39.9 %copy.19 = bf16[1,3,128,8192]{2,1,0,3:T(4,128)(2,1)} copy(bf16[1,3,128,8192]{2,3,1,0:T(8,128)(2,1)S(1)} %bitcast_select_fusion) | data formatting | bytes 12582912 | tf_op jit(solution)/shard_map/jit(_take)/select_n | solution.py:15
  221.3 5.6 all-to-all-start.1
  227.3 2.5 fusion.34
  229.8 7.6 while.5
  237.4 39.3 %custom-call.4 = f32[4,128,128]{1,2,0:T(8,128)S(1)} custom-call(f32[4,128,128]{2,1,0:T(8,128)S(1)} %get-tuple-element.32), custom_call_target="InvertDiagBlocksLowerTriangular" | custom-call | tf_op jit(solution)/shard_map/jit(_solve_triangular)/triangular_solve | solution.py:40
  276.8 43.3 %all-to-all-done.1 = bf16[1,3,128,8192]{2,1,0,3:T(4,128)(2,1)} async-done(((bf16[1,3,128,8192]{2,1,0,3:T(4,128)(2,1)}), bf16[1,3,128,8192]{2,1,0,3:T(4,128)(2,1)}, u32[]{:S(2)}, u32[]{:S(2)}) %all-to-all-start.1) | async-done | bytes 6291488 | tf_op jit(solution)/shard_map/all_to_all | solution.py:24
  320.1 4.3 copy.20
  325.5 4.5 copy-done.1
  332.3 5.4 copy.23
  346.7 3.0 fusion.18
  352.6 11.7 %while.6 = (s32[]{:T(128)}, f32[512,512]{1,0:T(8,128)}, s32[4,2]{0,1:T(2,128)S(1)}, f32[4,128,128]{2,1,0:T(8,128)S(1)}, s32[]{:T(128)}) while((s32[]{:T(128)}, f32[512,512]{1,0:T(8,128)}, s32[4,2]{0,1:T(2,128)S(1)}, f32[4,128,128]{2,1,0:T(8,128)S(1)}, s32[]{:T(128)}) %tuple.53), condition=%wide.while_cond.1.clone, body=%wide.while_body.1.clone.sunk | while | flops 2 | bytes 131189 | solution.py:40
  365.0 40.1 %custom-call.5 = f32[4,128,128]{1,2,0:T(8,128)S(1)} custom-call(f32[4,128,128]{2,1,0:T(8,128)} %copy-done.8), custom_call_target="InvertDiagBlocksLowerTriangular" | custom-call | tf_op jit(solution)/shard_map/jit(_solve_triangular)/triangular_solve | solution.py:40
  407.0 12.7 %copy.21 = f32[1,3,4,128,2048]{4,3,2,1,0:T(8,128)} copy(f32[1,3,4,128,2048]{3,4,2,1,0:T(8,128)} %copy-done.1) | data formatting | bytes 25165824 | tf_op jit(solution)/shard_map/convert_element_type | solution.py:33
  419.7 161.3 %all-gather.8.cloned.1.call-done = bf16[4096,2048]{1,0:T(8,128)(2,1)} async-done(((bf16[512,2048]{1,0:T(8,128)(2,1)}), bf16[4096,2048]{1,0:T(8,128)(2,1)}) %all-gather.8.cloned.1.call-update) | async-done | bytes 16777232 | tf_op jit(solution)/shard_map/all_gather | solution.py:9
  581.0 9.5 %reduce_sum.28 = bf16[512,2048]{1,0:T(8,128)(2,1)S(1)} reduce(bf16[8,512,2048]{2,1,0:T(8,128)(2,1)} %bitcast.126, bf16[]{:T(256)} %constant.67.clone.1), dimensions={0}, to_apply=%region_0.0 | reduce | flops 7340032 | bytes 18874370 | tf_op jit(solution)/shard_map/reduce_sum | solution.py:9
  590.5 5.0 fusion.58
  595.5 6.7 sub.25
  613.4 3.0 fusion.15
  619.2 225.6 %all-gather.10.cloned.1.call-done = bf16[4096,2048]{1,0:T(8,128)(2,1)} async-done(((bf16[512,2048]{1,0:T(8,128)(2,1)}), bf16[4096,2048]{1,0:T(8,128)(2,1)}) %all-gather.10.cloned.1.call-update) | async-done | bytes 16777232 | tf_op jit(solution)/shard_map/all_gather | solution.py:9
  844.9 11.0 %reduce_sum.29 = bf16[512,2048]{1,0:T(8,128)(2,1)} reduce(bf16[8,512,2048]{2,1,0:T(8,128)(2,1)} %bitcast.127, bf16[]{:T(256)} %constant.67.clone.1), dimensions={0}, to_apply=%region_1.3 | reduce | flops 7340032 | bytes 18874370 | tf_op jit(solution)/shard_map/reduce_sum | solution.py:9
  855.8 5.6 fusion.59
  861.5 12.5 %fusion.1 = bf16[1,3,512,2048]{3,2,1,0:T(8,128)(2,1)} fusion(f32[1,3,512,2048]{3,2,1,0:T(8,128)S(1)} %bitcast.124, f32[1,3,512,2048]{3,2,1,0:T(8,128)} %bitcast.119, f32[1,3,4,128,2048]{4,3,2,1,0:T(8,128)} %copy.21), kind=kLoop, calls=%fused_computation.8 | loop fusion | flops 9437184 | bytes 44040192 | tf_op jit(solution)/shard_map/convert_element_type | solution.py:46
  874.0 5.0 fusion.26
  (78 shorter events, 52.2 us)
Async XLA Ops:
  17.9 6.0 copy-start.7
  17.9 7.0 copy-start.9
  17.9 116.5 %all-to-all-start = ((bf16[1,3,512,2048]{3,1,0,2:T(4,128)(2,1)}), bf16[1,3,512,2048]{3,1,0,2:T(4,128)(2,1)}, u32[]{:S(2)}, u32[]{:S(2)}) async-start(bf16[1,3,512,2048]{3,1,0,2:T(4,128)(2,1)} %copy.14), calls=%async_computation | async-start | bytes 16777216 | tf_op jit(solution)/shard_map/all_to_all | solution.py:26
  23.7 203.6 %all-gather.6.cloned.1.call-start = ((), (), s32[]{:S(2)}) async-start(), calls=%async_computation.2 | async-start | bytes 3932160 | tf_op jit(solution)/shard_map/all_gather | solution.py:21
  221.3 98.8 %all-to-all-start.1 = ((bf16[1,3,128,8192]{2,1,0,3:T(4,128)(2,1)}), bf16[1,3,128,8192]{2,1,0,3:T(4,128)(2,1)}, u32[]{:S(2)}, u32[]{:S(2)}) async-start(bf16[1,3,128,8192]{2,1,0,3:T(4,128)(2,1)} %copy.19), calls=%async_computation.1 | async-start | bytes 16777216 | tf_op jit(solution)/shard_map/all_to_all | solution.py:24
  226.9 354.0 %all-gather.8.cloned.1.call-start = ((), (), s32[]{:S(2)}) async-start(), calls=%async_computation.3 | async-start | bytes 18874368 | tf_op jit(solution)/shard_map/all_gather | solution.py:9
  237.4 39.3 %copy-start.6 = (f32[512,512]{1,0:T(8,128)}, f32[512,512]{1,0:T(8,128)S(1)}, u32[]{:S(2)}) copy-start(f32[512,512]{1,0:T(8,128)S(1)} %get-tuple-element.163) | copy-start | bytes 3145732
  325.5 4.5 copy-start.1
  337.7 5.8 copy-start.3
  350.7 54.4 %copy-start.5 = (bf16[1,3,512,2,512]{4,2,3,1,0:T(8,128)(2,1)S(1)}, bf16[1,3,512,2,512]{4,2,3,1,0:T(8,128)(2,1)}, u32[]{:S(2)}) copy-start(bf16[1,3,512,2,512]{4,2,3,1,0:T(8,128)(2,1)} %all-gather.6.cloned.1.call-done) | copy-start | bytes 9437188
  352.5 492.3 %all-gather.10.cloned.1.call-start = ((), (), s32[]{:S(2)}) async-start(), calls=%async_computation.4 | async-start | bytes 18874368 | tf_op jit(solution)/shard_map/all_gather | solution.py:9
  364.3 0.7 copy-start.8
  590.4 5.0 copy-start
  595.5 8.3 copy-start.2
  861.4 12.5 %copy-start.4 = (bf16[512,2048]{1,0:T(8,128)(2,1)S(1)}, bf16[512,2048]{1,0:T(8,128)(2,1)}, u32[]{:S(2)}) copy-start(bf16[512,2048]{1,0:T(8,128)(2,1)} %reduce_sum.29) | copy-start | bytes 6291460
Sparse Core Ops, SparseCore 0:
  26.1 49.0 all-gather.5
  352.7 228.2 all-gather.7
  619.4 225.4 all-gather.9
